TPU v7x, 256 devices: a whole 4x4x8 slice. The times are simulated.
256 devices in a mesh: col: 8 (over y, core), row: 32 (over z, x).
Axes of the slice: x: 4, y: 4, z: 8, core: 2. Of those that a mesh axis runs over, the one named last changes fastest.
Arguments:
- column_table: float32 [262144, 512], P('row', 'col'), may hold values from -3 to 3
- bag_rows: int32 [1024, 32], P('row'), may hold values from 0 to 262143
Outputs:
- row_table: float32 [32, 8192, 512], P(None, ('col', 'row'))
- pooled: float32 [1024, 512], P('row', 'col')
Inputs may be any that keep to these rules, and one draw needn't show every extreme that they name: `bag_rows`: row indices of the table; a few rows are named far more often than the rest.
All inputs are finite; a program needn't handle non-finite values.
Results may differ from a plain program's by a relative error of at most 0.000078.
Values sent between devices are 32-bit elements; how exact they have to be, the bound alone decides.
A program may use at most 64 MiB of HBM per device.

v0:
```python
import math

import jax
import jax.numpy as jnp
from jax import lax
from jax.sharding import PartitionSpec as P


def copy_for_each(array, axis):
    copies = jnp.broadcast_to(array, (lax.axis_size(axis), *array.shape))
    return lax.all_to_all(copies, axis, split_axis=0, concat_axis=0, tiled=True)


def joined_along(blocks, dim):
    blocks = jnp.moveaxis(blocks, 0, dim)
    dims = blocks.shape
    return blocks.reshape(*dims[:dim], dims[dim] * dims[dim + 1], *dims[dim + 2 :])


def gather_directly(array, axis, dim):
    blocks = copy_for_each(array, axis)
    return joined_along(blocks, dim)


def split_up(array, dim, devices):
    dims = array.shape
    blocks = array.reshape(*dims[:dim], devices, dims[dim] // devices, *dims[dim + 1 :])
    return jnp.moveaxis(blocks, dim, 0)


def sum_at_owner(array, axis, dim):
    blocks = split_up(array, dim, lax.axis_size(axis))
    arrived = lax.all_to_all(blocks, axis, split_axis=0, concat_axis=0, tiled=True)
    return arrived.sum(axis=0)


def pooling(positions, table_rows):
    row_count = table_rows.shape[0]
    bag_count = positions.shape[0]
    block_rows = math.gcd(row_count, 512)
    turns = row_count // block_rows
    running = jnp.zeros((bag_count, table_rows.shape[1]), jnp.float32)
    tile_ids = jnp.arange(block_rows, dtype=jnp.int32)

    def advance(turn, carried):
        offset = turn * block_rows
        within = positions - offset
        matches = within[:, :, None] == tile_ids[None, None, :]
        counts = jnp.sum(matches.astype(jnp.float32), axis=1)
        table_block = lax.dynamic_slice_in_dim(table_rows, offset, block_rows, 0)
        return carried + jnp.dot(
            counts, table_block, precision=lax.Precision.HIGHEST, preferred_element_type=jnp.float32
        )

    return lax.fori_loop(0, turns, advance, running)


def per_device(column_table, bag_rows):
    row_groups = lax.axis_size("row")
    col_groups = lax.axis_size("col")
    block_len, col_width = column_table.shape
    full_width = col_width * col_groups
    span = block_len // (col_groups * row_groups)
    row_index = lax.axis_index("row")
    col_index = lax.axis_index("col")
    every_bag = gather_directly(bag_rows, "row", 0)
    sectioned = column_table.reshape(col_groups, row_groups, span, col_width)
    moved = lax.all_to_all(
        lax.all_to_all(sectioned, "col", split_axis=0, concat_axis=3, tiled=True),
        "row",
        split_axis=1,
        concat_axis=0,
        tiled=True,
    )
    row_table = moved.reshape(row_groups, span, full_width)
    group_of = every_bag // block_len
    inside = every_bag % block_len
    holder = col_index * row_groups + row_index
    held = inside // span == holder
    positions = jnp.where(held, group_of * span + inside % span, -1)
    partial_value = pooling(positions, row_table.reshape(row_groups * span, full_width))
    narrowed = sum_at_owner(partial_value, "col", 1)
    pooled = sum_at_owner(narrowed, "row", 0)
    return (row_table, pooled)


def solution(mesh):
    return jax.shard_map(
        per_device,
        mesh=mesh,
        in_specs=(P("row", "col"), P("row", None)),
        out_specs=(P(None, ("col", "row"), None), P("row", "col")),
        check_vma=False,
    )
```

profile of v0, /device:TPU:1, one launch (start us, length us, event | category | flops | bytes accessed | tf_op | source)
XLA Modules:
  0.0 229.6 jit_solution(11231773063323237859)
XLA Ops:
  0.6 3.8 %copy.19 = f32[8192,64]{1,0:T(8,128)} copy(f32[8192,64]{0,1:T(8,128)} %param.4) | data formatting | bytes 4194304 | tf_op args[0]
  4.4 7.2 %reshape.36 = f32[8,1,65536]{2,1,0:T(1,128)} reshape(f32[8,32,32,64]{3,2,1,0:T(8,128)} %bitcast.32) | data formatting | bytes 4194304
  11.6 6.8 %all-to-all-start = ((f32[8,1,65536]{2,1,0:T(1,128)}), f32[8,1,65536]{2,1,0:T(1,128)S(1)}, u32[]{:S(2)}, u32[]{:S(2)}) async-start(f32[8,1,65536]{2,1,0:T(1,128)} %reshape.36), calls=%async_computation | async-start | bytes 4194304 | tf_op jit(solution)/shard_map/all_to_all | solution.py:69
  19.4 25.3 %all-to-all-done = f32[8,1,65536]{2,1,0:T(1,128)S(1)} async-done(((f32[8,1,65536]{2,1,0:T(1,128)}), f32[8,1,65536]{2,1,0:T(1,128)S(1)}, u32[]{:S(2)}, u32[]{:S(2)}) %all-to-all-start) | async-done | bytes 2097184 | tf_op jit(solution)/shard_map/all_to_all | solution.py:69
  44.7 10.3 %all-to-all-start.2 = ((s32[32,1,1024]{2,1,0:T(1,128)}), s32[32,1,1024]{2,1,0:T(1,128)S(1)}, u32[]{:S(2)}, u32[]{:S(2)}) async-start(s32[32,1,1024]{2,1,0:T(1,128)} %reshape.38), calls=%async_computation.2 | async-start | bytes 262144 | tf_op jit(solution)/shard_map/all_to_all | solution.py:11
  55.5 7.2 %reduce = f32[8,65536]{1,0:T(8,128)S(1)} reduce(f32[8,1,65536]{2,1,0:T(1,128)} %copy-done, f32[]{:T(128)} %broadcast.34), dimensions={1}, to_apply=%all_to_all.29.reduce_sub_computation | reduce | bytes 4194308 | tf_op jit(solution)/shard_map/all_to_all | solution.py:69
  62.7 3.6 %reshape.37 = f32[8,32,32,64]{3,2,1,0:T(8,128)} reshape(f32[8,65536]{1,0:T(8,128)S(1)} %reduce) | data formatting | bytes 4194304
  66.3 7.9 %copy.20 = f32[1,32,32,8,64]{4,3,2,1,0:T(8,128)} copy(f32[1,32,32,8,64]{4,2,1,3,0:T(8,128)} %bitcast.33) | data formatting | bytes 4194304 | tf_op jit(solution)/shard_map/all_to_all | solution.py:69
  74.2 4.8 %all_to_all.32 = f32[1,32,32,512]{3,2,1,0:T(8,128)} reshape(f32[1,32,32,8,64]{4,3,2,1,0:T(8,128)} %copy.20) | data formatting | bytes 4194304 | tf_op jit(solution)/shard_map/all_to_all | solution.py:69
  79.0 9.3 %all-to-all-start.1 = ((f32[1,32,32,512]{3,2,0,1:T(8,128)}), f32[1,32,32,512]{3,2,0,1:T(8,128)}, u32[]{:S(2)}, u32[]{:S(2)}) async-start(f32[1,32,32,512]{3,2,0,1:T(8,128)} %bitcast.3), calls=%async_computation.1 | async-start | bytes 4194304 | tf_op jit(solution)/shard_map/all_to_all | solution.py:68
  90.0 1.0 fusion.7
  91.0 45.1 %all-to-all-done.1 = f32[1,32,32,512]{3,2,0,1:T(8,128)} async-done(((f32[1,32,32,512]{3,2,0,1:T(8,128)}), f32[1,32,32,512]{3,2,0,1:T(8,128)}, u32[]{:S(2)}, u32[]{:S(2)}) %all-to-all-start.1) | async-done | bytes 2097184 | tf_op jit(solution)/shard_map/all_to_all | solution.py:68
  136.1 34.6 %while.14 = (s32[]{:T(128)}, f32[1024,512]{1,0:T(8,128)}, s32[1024,32]{1,0:T(8,128)S(1)}, f32[1024,512]{1,0:T(8,128)}, s32[]{:T(128)}, /*index=5*/s32[]{:T(128)}, s32[]{:T(128)}, s32[]{:T(128)}) while((s32[]{:T(128)}, f32[1024,512]{1,0:T(8,128)}, s32[1024,32]{1,0:T(8,128)S(1)}, f32[1024,512]{1,0:T(8,128)}, s32[]{:T(128)}, ...), condition=%wide.region_2.3_spmd.clone, body=%wide.region_0.2_spmd.clone.sunk | while | flops 3272114176 | bytes 9830549 | solution.py:55
  136.2 11.1 %convert_reduce_fusion.2 = f32[1024,512]{1,0:T(8,128)S(1)} fusion(s32[1024,32]{1,0:T(8,128)S(1)} %broadcast_subtract_fusion.2), kind=kLoop, calls=%fused_computation.2.clone.1 | loop fusion | flops 49807360 | bytes 2228224 | tf_op jit(solution)/shard_map/while/body/eval_jaxpr/reduce_sum | solution.py:49
  147.3 6.0 %select_add_fusion.2 = f32[1024,512]{1,0:T(8,128)} fusion(f32[1024,512]{1,0:T(8,128)} %get-tuple-element.156, f32[1024,512]{1,0:T(8,128)S(1)} %convert_reduce_fusion.2, f32[1024,512]{1,0:T(8,128)} %get-tuple-element.166, s32[]{:T(128)S(6)} %select_n.56, pred[]{:T(512)S(6)} %compare.9), kind=kOutput, calls=%fused_computation.3.clone.1 | convolution fusion | flops 3222274048 | bytes 7340037 | tf_op jit(solution)/shard_map/while/body/eval_jaxpr/dot_general | solution.py:51
  153.3 11.1 %convert_reduce_fusion.2 = f32[1024,512]{1,0:T(8,128)S(1)} fusion(s32[1024,32]{1,0:T(8,128)S(1)} %broadcast_subtract_fusion.2), kind=kLoop, calls=%fused_computation.2.clone.1 | loop fusion | flops 49807360 | bytes 2228224 | tf_op jit(solution)/shard_map/while/body/eval_jaxpr/reduce_sum | solution.py:49
  164.4 6.3 %select_add_fusion.2 = f32[1024,512]{1,0:T(8,128)} fusion(f32[1024,512]{1,0:T(8,128)} %get-tuple-element.156, f32[1024,512]{1,0:T(8,128)S(1)} %convert_reduce_fusion.2, f32[1024,512]{1,0:T(8,128)} %get-tuple-element.166, s32[]{:T(128)S(6)} %select_n.56, pred[]{:T(512)S(6)} %compare.9), kind=kOutput, calls=%fused_computation.3.clone.1 | convolution fusion | flops 3222274048 | bytes 7340037 | tf_op jit(solution)/shard_map/while/body/eval_jaxpr/dot_general | solution.py:51
  170.7 2.9 %copy.22 = f32[1024,512]{0,1:T(8,128)} copy(f32[1024,512]{1,0:T(8,128)} %get-tuple-element.96) | data formatting | bytes 4194304 | tf_op jit(solution)/shard_map/while | solution.py:55
  173.6 33.0 %all_to_all.42 = f32[8,1024,64]{1,2,0:T(8,128)S(1)} all-to-all(f32[8,1024,64]{1,2,0:T(8,128)} %bitcast.34), channel_id=1, replica_groups=mesh['col'=8,'row'=32] {'col'}, dimensions={0} | all-to-all | bytes 4194304 | tf_op jit(solution)/shard_map/all_to_all | solution.py:33
  206.9 1.0 reshape.40
  207.9 5.7 %all-to-all-start.4 = ((f32[32,1,2048]{2,1,0:T(1,128)}), f32[32,1,2048]{2,1,0:T(1,128)S(1)}, u32[]{:S(2)}, u32[]{:S(2)}) async-start(f32[32,1,2048]{2,1,0:T(1,128)} %reshape.40), calls=%async_computation.4 | async-start | bytes 524288 | tf_op jit(solution)/shard_map/all_to_all | solution.py:33
  213.6 10.6 %all-to-all-done.4 = f32[32,1,2048]{2,1,0:T(1,128)S(1)} async-done(((f32[32,1,2048]{2,1,0:T(1,128)}), f32[32,1,2048]{2,1,0:T(1,128)S(1)}, u32[]{:S(2)}, u32[]{:S(2)}) %all-to-all-start.4) | async-done | bytes 262176 | tf_op jit(solution)/shard_map/all_to_all | solution.py:33
  224.2 1.3 reduce.2
  226.4 3.2 %copy.31 = f32[32,32,512]{2,1,0:T(8,128)} copy(f32[32,32,512]{2,1,0:T(8,128)} %bitcast.4) | data formatting | bytes 4194304
  (18 shorter events, 4.4 us)
Async XLA Ops:
  11.6 6.8 %copy-start.1 = (s32[32,32]{1,0:T(8,128)S(1)}, s32[32,32]{1,0:T(8,128)}, u32[]{:S(2)}) copy-start(s32[32,32]{1,0:T(8,128)} %param.5) | copy-start | bytes 12292
  11.6 33.1 %all-to-all-start = ((f32[8,1,65536]{2,1,0:T(1,128)}), f32[8,1,65536]{2,1,0:T(1,128)S(1)}, u32[]{:S(2)}, u32[]{:S(2)}) async-start(f32[8,1,65536]{2,1,0:T(1,128)} %reshape.36), calls=%async_computation | async-start | bytes 4194304 | tf_op jit(solution)/shard_map/all_to_all | solution.py:69
  44.7 10.3 %copy-start = (f32[8,1,65536]{2,1,0:T(1,128)}, f32[8,1,65536]{2,1,0:T(1,128)S(1)}, u32[]{:S(2)}) copy-start(f32[8,1,65536]{2,1,0:T(1,128)S(1)} %all-to-all-done) | copy-start | bytes 6291460
  44.7 34.3 %all-to-all-start.2 = ((s32[32,1,1024]{2,1,0:T(1,128)}), s32[32,1,1024]{2,1,0:T(1,128)S(1)}, u32[]{:S(2)}, u32[]{:S(2)}) async-start(s32[32,1,1024]{2,1,0:T(1,128)} %reshape.38), calls=%async_computation.2 | async-start | bytes 262144 | tf_op jit(solution)/shard_map/all_to_all | solution.py:11
  79.0 57.1 %all-to-all-start.1 = ((f32[1,32,32,512]{3,2,0,1:T(8,128)}), f32[1,32,32,512]{3,2,0,1:T(8,128)}, u32[]{:S(2)}, u32[]{:S(2)}) async-start(f32[1,32,32,512]{3,2,0,1:T(8,128)} %bitcast.3), calls=%async_computation.1 | async-start | bytes 4194304 | tf_op jit(solution)/shard_map/all_to_all | solution.py:68
  207.9 16.3 %all-to-all-start.4 = ((f32[32,1,2048]{2,1,0:T(1,128)}), f32[32,1,2048]{2,1,0:T(1,128)S(1)}, u32[]{:S(2)}, u32[]{:S(2)}) async-start(f32[32,1,2048]{2,1,0:T(1,128)} %reshape.40), calls=%async_computation.4 | async-start | bytes 524288 | tf_op jit(solution)/shard_map/all_to_all | solution.py:33
where the time goes:
time: 231 us; the launch traced here: 230 us
  waiting for transfers between devices  81.1 us (35%)
  local copies, waits for them, and re-layouts  37 us (16%)
  other arithmetic  33.5 us (15%)
  blocking collectives  33 us (14%)
  starting transfers between devices  32.1 us (14%)
  matrix products  12.2 us (5%)
    all_to_all x1, waiting for transfers between devices, per_device(): lax.all_to_all(lax.all_to_all(sectioned, 'col', split_axis=0, concat_axis...  45.1 us
    all_to_all x1, blocking collectives, sum_at_owner(): lax.all_to_all(blocks, axis, split_axis=0, concat_axis=0, tiled=True)  33 us
    all_to_all x1, waiting for transfers between devices, per_device(): lax.all_to_all(sectioned, 'col', split_axis=0, concat_axis=3, tiled=True)  25.3 us
    reduce_sum x2, other arithmetic, advance(): counts = jnp.sum(matches.astype(jnp.float32), axis=1)  22.2 us
    unnamed x12, local copies, waits for them, and re-layouts  20.1 us
    all_to_all x3, local copies, waits for them, and re-layouts, per_device(): lax.all_to_all(sectioned, 'col', split_axis=0, concat_axis=3, tiled=True)  13.2 us
    dot_general x2, matrix products, advance(): jnp.dot(counts, table_block, precision=lax.Precision.HIGHEST, preferred_e...  12.2 us
    all_to_all x1, waiting for transfers between devices, sum_at_owner(): lax.all_to_all(blocks, axis, split_axis=0, concat_axis=0, tiled=True)  10.6 us
  transfers between devices with their start and end apart: 4, of which 3 were waited for; matrix products, arithmetic and copies ran while one was open for 10% of the time, Pallas kernels for 0%

commit v1 on v0

v1 whole, which is shorter than its diff:
```python
import functools

import jax
import jax.numpy as jnp
from jax import lax
from jax.experimental import pallas as pl
from jax.experimental.pallas import tpu as pltpu
from jax.sharding import PartitionSpec as P

MESH = pl.DeviceIdType.MESH
LANES = 128
BAG_LEN = 32


def kernel(
    zn, xn, span, table_ref, bags_ref, out_ref, pooled_ref,
    raw, flat, ids, near, part2, part, x_in, held, z_in, spot,
    load_sem, pair_send, pair_recv, ids_send, ids_recv, move_send, move_recv,
    x_send, x_recv, z_send, z_recv, spot_sem, own_sem,
):
    rows = zn * xn
    half, length = table_ref.shape
    width = rows * span
    chunks = length // width
    yn = chunks // 2
    col = lax.axis_index("col")
    row = lax.axis_index("row")
    y, core = col // 2, col % 2
    z, x = row // xn, row % xn
    sibling = y * 2 + (1 - core)

    def chunk_at(i, parity):
        c = lax.rem(y + i, yn) * 2 + parity
        return c, pl.ds(pl.multiple_of(c * width, LANES), width)

    def local_load(n):
        c, lanes = chunk_at(n % yn, core if n < yn else 1 - core)
        mine = pl.ds(pl.multiple_of(core * half, 8), half)
        return pltpu.make_async_copy(table_ref.at[:, lanes], raw.at[mine, lanes], load_sem.at[n])

    def pair_copy(n):
        c, lanes = chunk_at(n % yn, 1 - core if n < yn else core)
        mine = pl.ds(pl.multiple_of(core * half, 8), half)
        return pltpu.make_async_remote_copy(
            src_ref=table_ref.at[:, lanes], dst_ref=raw.at[mine, lanes],
            send_sem=pair_send.at[n], recv_sem=pair_recv.at[n],
            device_id=(sibling, row), device_id_type=MESH,
        )

    for n in range(chunks):
        pair_copy(n).start()
        local_load(n).start()

    bags = bags_ref[...]
    eighth = bags.shape[0] // 4
    own_ids = pl.ds(pl.multiple_of(row * eighth, 8), eighth)
    ids[own_ids, :] = jnp.concatenate([bags[q * eighth : (q + 1) * eighth] for q in range(4)], axis=1)
    flat[pl.ds(length, 8), :] = jnp.zeros((8, LANES), jnp.float32)

    def transpose(n):
        c, lanes = chunk_at(n % yn, core if n < yn else 1 - core)
        local_load(n).wait()
        pair_copy(n).wait_recv()

        def step(t, carry):
            at = pl.ds(pl.multiple_of(c * width + t * LANES, LANES), LANES)
            flat[at, :] = raw[:, at].T
            return carry

        lax.fori_loop(0, width // LANES, step, 0)

    def block(c, rr):
        return flat.at[pl.ds(pl.multiple_of(c * width + rr * span, 8), span)]

    landing = out_ref.at[row, :, pl.ds(pl.multiple_of(y * LANES, LANES), LANES)]

    def send_blocks(n):
        c, _ = chunk_at(n, core)

        def step(t, carry):
            rr = lax.rem(z + t // xn, zn) * xn + lax.rem(x + t % xn, xn)
            pltpu.make_async_remote_copy(
                src_ref=block(c, rr), dst_ref=landing, send_sem=move_send, recv_sem=move_recv,
                device_id=(c, rr), device_id_type=MESH,
            ).start()
            return carry

        lax.fori_loop(1 if n == 0 else 0, rows, step, 0)

    def send_ids(t, carry):
        rr = lax.rem(row + t, rows)
        pltpu.make_async_remote_copy(
            src_ref=ids.at[own_ids], dst_ref=ids.at[own_ids], send_sem=ids_send, recv_sem=ids_recv,
            device_id=(col, rr), device_id_type=MESH,
        ).start()
        return carry

    transpose(0)
    lax.fori_loop(1, rows, send_ids, 0)
    for n in range(yn):
        if n + 1 < yn:
            transpose(n + 1)
        else:
            transpose(yn)
        send_blocks(n)
    own = pltpu.make_async_copy(block(col, row), landing, own_sem)
    own.start()
    for n in range(yn + 1, chunks):
        transpose(n)

    others = (rows - 1) * eighth
    pltpu.make_async_copy(ids.at[pl.ds(0, others)], ids.at[pl.ds(0, others)], ids_recv).wait()
    every = ids[...]
    near[...] = jnp.where(every // length == row, every % length, length)
    to_scalar = pltpu.make_async_copy(near, spot, spot_sem)
    to_scalar.start()
    to_scalar.wait()

    def gather(t, carry):
        for q in range(2):
            sums = [None] * 4
            for l in range(BAG_LEN):
                at = spot[t, core * (2 * BAG_LEN) + q * BAG_LEN + l]
                value = flat[pl.ds(at, 1), :]
                sums[l % 4] = value if sums[l % 4] is None else sums[l % 4] + value
            part2[q, pl.ds(t, 1), :] = (sums[0] + sums[1]) + (sums[2] + sums[3])
        return carry

    lax.fori_loop(0, rows * eighth, gather, 0)

    low = lax.broadcasted_iota(jnp.int32, (8, LANES), 1) < half

    def split(s, carry):
        at = pl.ds(pl.multiple_of(s * 8, 8), 8)
        first, second = part2[0, at, :], part2[1, at, :]
        part[s % xn, s // xn, 0] = jnp.where(low, first, pltpu.roll(second, half, 1))
        part[s % xn, s // xn, 1] = jnp.where(low, pltpu.roll(first, half, 1), second)
        return carry

    lax.fori_loop(0, rows, split, 0)

    for d in range(1, xn):
        xx = lax.rem(x + d, xn)
        pltpu.make_async_remote_copy(
            src_ref=part.at[xx], dst_ref=x_in.at[x], send_sem=x_send, recv_sem=x_recv,
            device_id=(col, z * xn + xx), device_id_type=MESH,
        ).start()
    x_rest = part.at[pl.ds(0, xn - 1)]
    pltpu.make_async_copy(x_rest, x_rest, x_recv).wait()
    total = part[x]
    for d in range(1, xn):
        total = total + x_in[lax.rem(x + d, xn)]
    held[...] = total

    for d in range(zn):
        zz = lax.rem(z + d, zn)
        for e in range(2):
            if d == 0 and e == 0:
                continue
            kk = core if e == 0 else 1 - core
            pltpu.make_async_remote_copy(
                src_ref=held.at[zz, kk], dst_ref=z_in.at[z * 2 + core], send_sem=z_send, recv_sem=z_recv,
                device_id=(y * 2 + kk, zz * xn + x), device_id_type=MESH,
            ).start()
    z_in[z * 2 + core] = held[z, core]
    z_rest = z_in.at[pl.ds(0, 2 * zn - 1)]
    pltpu.make_async_copy(z_rest, z_rest, z_recv).wait()
    for k in range(2):
        total = z_in[k]
        for d in range(1, zn):
            total = total + z_in[d * 2 + k]
        pooled_ref[pl.ds(k * 16, 8), :] = total[:, :half]
        pooled_ref[pl.ds(k * 16 + 8, 8), :] = pltpu.roll(total, half, 1)[:, :half]

    own.wait()
    moved = flat.at[pl.ds(0, (yn * rows - 1) * span)]
    pltpu.make_async_copy(moved, moved, move_recv).wait()
    pltpu.make_async_copy(moved, moved, move_send).wait()
    sent_ids = ids.at[pl.ds(0, others)]
    pltpu.make_async_copy(sent_ids, sent_ids, ids_send).wait()
    pltpu.make_async_copy(x_rest, x_rest, x_send).wait()
    pltpu.make_async_copy(z_rest, z_rest, z_send).wait()
    for n in range(chunks):
        pair_copy(n).wait_send()


def per_device(zn, xn, column_table, bag_rows):
    rows = zn * xn
    chunks = lax.axis_size("col")
    length, half = column_table.shape
    span = length // (rows * chunks)
    f32 = jnp.float32
    dma = pltpu.SemaphoreType.DMA
    row_table, pooled = pl.pallas_call(
        functools.partial(kernel, zn, xn, span),
        out_shape=[
            jax.ShapeDtypeStruct((rows, span, half * chunks), f32),
            jax.ShapeDtypeStruct((bag_rows.shape[0], half), f32),
        ],
        in_specs=[pl.BlockSpec(memory_space=pl.ANY), pl.BlockSpec(memory_space=pltpu.VMEM)],
        out_specs=[pl.BlockSpec(memory_space=pl.ANY), pl.BlockSpec(memory_space=pltpu.VMEM)],
        scratch_shapes=[
            pltpu.VMEM((2 * half, length), f32),
            pltpu.VMEM((length + 8, LANES), f32),
            pltpu.VMEM((rows * 8, LANES), jnp.int32),
            pltpu.VMEM((rows * 8, LANES), jnp.int32),
            pltpu.VMEM((2, rows * 8, LANES), f32),
            pltpu.VMEM((xn, zn, 2, 8, LANES), f32),
            pltpu.VMEM((xn, zn, 2, 8, LANES), f32),
            pltpu.VMEM((zn, 2, 8, LANES), f32),
            pltpu.VMEM((zn * 2, 8, LANES), f32),
            pltpu.SMEM((rows * 8, LANES), jnp.int32),
            dma((chunks,)), dma((chunks,)), dma((chunks,)),
            dma, dma, dma, dma, dma, dma, dma, dma, dma, dma,
        ],
        compiler_params=pltpu.CompilerParams(has_side_effects=True, vmem_limit_bytes=40 * 1024 * 1024),
    )(column_table.T, bag_rows)
    return row_table, pooled


def solution(mesh):
    rows = mesh.shape["row"]
    xn = 4 if rows == 32 else 2
    return jax.shard_map(
        functools.partial(per_device, rows // xn, xn),
        mesh=mesh,
        in_specs=(P("row", "col"), P("row", None)),
        out_specs=(P(None, ("col", "row"), None), P("row", "col")),
        check_vma=False,
    )
```

time: 231 us -> 90.6 us (0.39)
  Pallas kernels: 0 us -> 85.5 us
  waiting for transfers between devices: 81.1 us -> 0 us
  other arithmetic: 33.5 us -> 0 us
  blocking collectives: 33 us -> 0 us
  local copies, waits for them, and re-layouts: 37 us -> 4.23 us
  starting transfers between devices: 32.1 us -> 0 us
  matrix products: 12.2 us -> 0 us
    pallas_call x0 -> x1, Pallas kernels: none -> 85.5 us  [per_device(): pl.pallas_call(functools.partial(kernel, zn, xn, span), out_shape=[jax.Sh...]
    all_to_all x4 -> x0, waiting for transfers between devices: 81.1 us -> none  [the longest x1 45.1 us: per_device(): lax.all_to_all(lax.all_to_all(sectioned, 'col', split_axis=0, concat_axis...]
    all_to_all x1 -> x0, blocking collectives: 33 us -> none  [sum_at_owner(): lax.all_to_all(blocks, axis, split_axis=0, concat_axis=0, tiled=True)]
    all_to_all x4 -> x0, starting transfers between devices: 32.1 us -> none  [the longest x1 10.3 us: copy_for_each(): return lax.all_to_all(copies, axis, split_axis=0, concat_axis=0, tiled=True)]
    reduce_sum x4 -> x0, other arithmetic: 23 us -> none  [the longest x2 22.2 us: advance(): counts = jnp.sum(matches.astype(jnp.float32), axis=1)]
    unnamed x12 -> x6, local copies, waits for them, and re-layouts: 20.1 us -> 4.23 us
    all_to_all x4 -> x0, local copies, waits for them, and re-layouts: 13.8 us -> none  [the longest x3 13.2 us: per_device(): lax.all_to_all(sectioned, 'col', split_axis=0, concat_axis=3, tiled=True)]
    dot_general x2 -> x0, matrix products: 12.2 us -> none  [advance(): jnp.dot(counts, table_block, precision=lax.Precision.HIGHEST, preferred_e...]
  transfers between devices with their start and end apart: 4 -> 0, of which waited for: 3 -> 0; matrix products, arithmetic and copies ran while one was open for 10% -> 0% of each run, Pallas kernels for 0% -> 0%
where the time goes in v1:
time: 90.6 us; the launch traced here: 90.4 us
  Pallas kernels  85.5 us (94%)
  local copies, waits for them, and re-layouts  4.23 us (5%)
    pallas_call x1, Pallas kernels, per_device(): pl.pallas_call(functools.partial(kernel, zn, xn, span), out_shape=[jax.Sh...  85.5 us
    unnamed x6, local copies, waits for them, and re-layouts  4.23 us

profile of v1, /device:TPU:1, one launch (start us, length us, event | category | flops | bytes accessed | tf_op | source)
XLA Modules:
  0.0 90.4 jit_solution(9335432235506123327)
XLA Ops:
  0.6 0.0 copy-start
  0.6 1.6 %copy-done = f32[8192,64]{0,1:T(8,128)S(1)} copy-done((f32[8192,64]{0,1:T(8,128)S(1)}, f32[8192,64]{0,1:T(8,128)}, u32[]{:S(2)}) %copy-start) | copy-done | bytes 2097176
  2.2 0.0 copy-start.1
  2.2 0.7 copy-done.1
  2.9 85.5 %shard_map.41 = (f32[32,32,512]{2,1,0:T(8,128)S(1)}, f32[32,64]{1,0:T(8,128)S(1)}) custom-call(f32[64,8192]{1,0:T(8,128)S(1)} %bitcast.1, s32[32,32]{1,0:T(8,128)S(1)} %copy-done.1), custom_call_target="tpu_custom_call" | custom-call | tf_op jit(solution)/shard_map/pallas_call | solution.py:194
  88.5 1.3 %copy.6 = f32[32,32,512]{2,1,0:T(8,128)} copy(f32[32,32,512]{2,1,0:T(8,128)S(1)} %get-tuple-element.4) | data formatting | bytes 4194304
  89.8 0.6 copy.7
Async XLA Ops:
  0.6 1.6 %copy-start = (f32[8192,64]{0,1:T(8,128)S(1)}, f32[8192,64]{0,1:T(8,128)}, u32[]{:S(2)}) copy-start(f32[8192,64]{0,1:T(8,128)} %param.2) | copy-start | bytes 6291460
  2.2 0.7 copy-start.1

commit v2 on v1

--- a/solution.py
+++ b/solution.py
@@ -14,9 +14,9 @@
 
 def kernel(
     zn, xn, span, table_ref, bags_ref, out_ref, pooled_ref,
-    raw, flat, ids, near, part2, part, x_in, held, z_in, spot,
+    raw, flat, bags, ids, near, part2, part, x_in, held, z_in, spot,
     load_sem, pair_send, pair_recv, ids_send, ids_recv, move_send, move_recv,
-    x_send, x_recv, z_send, z_recv, spot_sem, own_sem,
+    x_send, x_recv, z_send, z_recv, spot_sem, own_sem, bags_sem,
 ):
     rows = zn * xn
     half, length = table_ref.shape
@@ -28,6 +28,27 @@
     y, core = col // 2, col % 2
     z, x = row // xn, row % xn
     sibling = y * 2 + (1 - core)
+    away = sorted(range(1, zn), key=lambda d: -min(d, zn - d))
+
+    barrier = pltpu.get_barrier_semaphore()
+
+    def greet(c, rr):
+        pl.semaphore_signal(barrier, inc=1, device_id=(c, rr), device_id_type=MESH)
+
+    def greet_plane(i, carry):
+        c = lax.rem(y + i, yn) * 2 + core
+        for dx in range(xn):
+            xx = lax.rem(x + dx, xn)
+            for dz in away + ([0] if dx else []):
+                greet(c, lax.rem(z + dz, zn) * xn + xx)
+        return carry
+
+    greet(sibling, row)
+    lax.fori_loop(0, yn, greet_plane, 0)
+    for dz in away:
+        greet(sibling, lax.rem(z + dz, zn) * xn + x)
+    for i in range(1, yn):
+        greet(lax.rem(y + i, yn) * 2 + core, row)
 
     def chunk_at(i, parity):
         c = lax.rem(y + i, yn) * 2 + parity
@@ -47,14 +68,18 @@
             device_id=(sibling, row), device_id_type=MESH,
         )
 
+    load_bags = pltpu.make_async_copy(bags_ref, bags, bags_sem)
+    load_bags.start()
+    for n in range(chunks):
+        local_load(n).start()
+
+    load_bags.wait()
+    eighth = bags.shape[0] // 4
+    own_ids = pl.ds(pl.multiple_of(row * eighth, 8), eighth)
+    ids[own_ids, :] = jnp.concatenate([bags[q * eighth : (q + 1) * eighth, :] for q in range(4)], axis=1)
+    pl.semaphore_wait(barrier, yn * rows - 1 + zn)
     for n in range(chunks):
         pair_copy(n).start()
-        local_load(n).start()
-
-    bags = bags_ref[...]
-    eighth = bags.shape[0] // 4
-    own_ids = pl.ds(pl.multiple_of(row * eighth, 8), eighth)
-    ids[own_ids, :] = jnp.concatenate([bags[q * eighth : (q + 1) * eighth] for q in range(4)], axis=1)
     flat[pl.ds(length, 8), :] = jnp.zeros((8, LANES), jnp.float32)
 
     def transpose(n):
@@ -77,15 +102,24 @@
     def send_blocks(n):
         c, _ = chunk_at(n, core)
 
-        def step(t, carry):
-            rr = lax.rem(z + t // xn, zn) * xn + lax.rem(x + t % xn, xn)
+        def send(rr):
             pltpu.make_async_remote_copy(
                 src_ref=block(c, rr), dst_ref=landing, send_sem=move_send, recv_sem=move_recv,
                 device_id=(c, rr), device_id_type=MESH,
             ).start()
+
+        def step(dx, carry):
+            xx = lax.rem(x + dx, xn)
+            for dz in away:
+                send(lax.rem(z + dz, zn) * xn + xx)
             return carry
 
-        lax.fori_loop(1 if n == 0 else 0, rows, step, 0)
+        def step_near(dx, carry):
+            send(z * xn + lax.rem(x + dx, xn))
+            return carry
+
+        lax.fori_loop(0, xn, step, 0)
+        lax.fori_loop(1 if n == 0 else 0, xn, step_near, 0)
 
     def send_ids(t, carry):
         rr = lax.rem(row + t, rows)
@@ -95,23 +129,20 @@
         ).start()
         return carry
 
+    lax.fori_loop(1, rows, send_ids, 0)
     transpose(0)
-    lax.fori_loop(1, rows, send_ids, 0)
-    for n in range(yn):
-        if n + 1 < yn:
-            transpose(n + 1)
-        else:
-            transpose(yn)
-        send_blocks(n)
-    own = pltpu.make_async_copy(block(col, row), landing, own_sem)
-    own.start()
-    for n in range(yn + 1, chunks):
+    transpose(1)
+    send_blocks(0)
+    transpose(2 % chunks)
+    send_blocks(1)
+    for n in range(3, chunks):
         transpose(n)
 
     others = (rows - 1) * eighth
     pltpu.make_async_copy(ids.at[pl.ds(0, others)], ids.at[pl.ds(0, others)], ids_recv).wait()
     every = ids[...]
-    near[...] = jnp.where(every // length == row, every % length, length)
+    every = jnp.where(every // length == row, every % length, length)
+    near[...] = jnp.where(core == 0, every, pltpu.roll(every, LANES // 2, 1))
     to_scalar = pltpu.make_async_copy(near, spot, spot_sem)
     to_scalar.start()
     to_scalar.wait()
@@ -120,7 +151,7 @@
         for q in range(2):
             sums = [None] * 4
             for l in range(BAG_LEN):
-                at = spot[t, core * (2 * BAG_LEN) + q * BAG_LEN + l]
+                at = spot[t, q * BAG_LEN + l]
                 value = flat[pl.ds(at, 1), :]
                 sums[l % 4] = value if sums[l % 4] is None else sums[l % 4] + value
             part2[q, pl.ds(t, 1), :] = (sums[0] + sums[1]) + (sums[2] + sums[3])
@@ -145,6 +176,8 @@
             src_ref=part.at[xx], dst_ref=x_in.at[x], send_sem=x_send, recv_sem=x_recv,
             device_id=(col, z * xn + xx), device_id_type=MESH,
         ).start()
+    for n in range(2, yn - 1):
+        send_blocks(n)
     x_rest = part.at[pl.ds(0, xn - 1)]
     pltpu.make_async_copy(x_rest, x_rest, x_recv).wait()
     total = part[x]
@@ -162,6 +195,10 @@
                 src_ref=held.at[zz, kk], dst_ref=z_in.at[z * 2 + core], send_sem=z_send, recv_sem=z_recv,
                 device_id=(y * 2 + kk, zz * xn + x), device_id_type=MESH,
             ).start()
+    if yn > 2:
+        send_blocks(yn - 1)
+    own = pltpu.make_async_copy(block(col, row), landing, own_sem)
+    own.start()
     z_in[z * 2 + core] = held[z, core]
     z_rest = z_in.at[pl.ds(0, 2 * zn - 1)]
     pltpu.make_async_copy(z_rest, z_rest, z_recv).wait()
@@ -197,11 +234,12 @@
             jax.ShapeDtypeStruct((rows, span, half * chunks), f32),
             jax.ShapeDtypeStruct((bag_rows.shape[0], half), f32),
         ],
-        in_specs=[pl.BlockSpec(memory_space=pl.ANY), pl.BlockSpec(memory_space=pltpu.VMEM)],
+        in_specs=[pl.BlockSpec(memory_space=pltpu.HBM)] * 2,
         out_specs=[pl.BlockSpec(memory_space=pl.ANY), pl.BlockSpec(memory_space=pltpu.VMEM)],
         scratch_shapes=[
             pltpu.VMEM((2 * half, length), f32),
             pltpu.VMEM((length + 8, LANES), f32),
+            pltpu.VMEM(bag_rows.shape, jnp.int32),
             pltpu.VMEM((rows * 8, LANES), jnp.int32),
             pltpu.VMEM((rows * 8, LANES), jnp.int32),
             pltpu.VMEM((2, rows * 8, LANES), f32),
@@ -211,9 +249,9 @@
             pltpu.VMEM((zn * 2, 8, LANES), f32),
             pltpu.SMEM((rows * 8, LANES), jnp.int32),
             dma((chunks,)), dma((chunks,)), dma((chunks,)),
-            dma, dma, dma, dma, dma, dma, dma, dma, dma, dma,
+            dma, dma, dma, dma, dma, dma, dma, dma, dma, dma, dma,
         ],
-        compiler_params=pltpu.CompilerParams(has_side_effects=True, vmem_limit_bytes=40 * 1024 * 1024),
+        compiler_params=pltpu.CompilerParams(has_side_effects=True, collective_id=0, vmem_limit_bytes=40 * 1024 * 1024),
     )(column_table.T, bag_rows)
     return row_table, pooled
 

time: 90.6 us -> 73.6 us (0.81)
  Pallas kernels: 85.5 us -> 68.5 us
    pallas_call x1, Pallas kernels: 85.5 us -> 68.5 us  [per_device(): pl.pallas_call(functools.partial(kernel, zn, xn, span), out_shape=[jax.Sh...]
where the time goes in v2:
time: 73.6 us; the launch traced here: 73.4 us
  Pallas kernels  68.5 us (93%)
  local copies, waits for them, and re-layouts  4.23 us (6%)
    pallas_call x1, Pallas kernels, per_device(): pl.pallas_call(functools.partial(kernel, zn, xn, span), out_shape=[jax.Sh...  68.5 us
    unnamed x6, local copies, waits for them, and re-layouts  4.23 us

profile of v2, /device:TPU:1, one launch (start us, length us, event | category | flops | bytes accessed | tf_op | source)
XLA Modules:
  0.0 73.4 jit_solution(7103605648929922270)
XLA Ops:
  0.6 0.0 copy-start
  0.6 1.6 %copy-done = f32[8192,64]{0,1:T(8,128)S(1)} copy-done((f32[8192,64]{0,1:T(8,128)S(1)}, f32[8192,64]{0,1:T(8,128)}, u32[]{:S(2)}) %copy-start) | copy-done | bytes 2097176
  2.2 0.0 copy-start.1
  2.2 0.7 copy-done.1
  2.9 68.5 %shard_map.41 = (f32[32,32,512]{2,1,0:T(8,128)S(1)}, f32[32,64]{1,0:T(8,128)S(1)}) custom-call(f32[64,8192]{1,0:T(8,128)S(1)} %bitcast.1, s32[32,32]{1,0:T(8,128)S(1)} %copy-done.1), custom_call_target="tpu_custom_call" | custom-call | tf_op jit(solution)/shard_map/pallas_call | solution.py:231
  71.5 1.3 %copy.6 = f32[32,32,512]{2,1,0:T(8,128)} copy(f32[32,32,512]{2,1,0:T(8,128)S(1)} %get-tuple-element.4) | data formatting | bytes 4194304
  72.8 0.6 copy.7
Async XLA Ops:
  0.6 1.6 %copy-start = (f32[8192,64]{0,1:T(8,128)S(1)}, f32[8192,64]{0,1:T(8,128)}, u32[]{:S(2)}) copy-start(f32[8192,64]{0,1:T(8,128)} %param.2) | copy-start | bytes 6291460
  2.2 0.7 copy-start.1

commit v3 on v2

--- a/solution.py
+++ b/solution.py
@@ -50,6 +50,9 @@
     for i in range(1, yn):
         greet(lax.rem(y + i, yn) * 2 + core, row)
 
+    def load_of_pair(n):
+        return n + yn if n < yn else n - yn
+
     def chunk_at(i, parity):
         c = lax.rem(y + i, yn) * 2 + parity
         return c, pl.ds(pl.multiple_of(c * width, LANES), width)
@@ -63,28 +66,28 @@
         c, lanes = chunk_at(n % yn, 1 - core if n < yn else core)
         mine = pl.ds(pl.multiple_of(core * half, 8), half)
         return pltpu.make_async_remote_copy(
-            src_ref=table_ref.at[:, lanes], dst_ref=raw.at[mine, lanes],
+            src_ref=raw.at[mine, lanes], dst_ref=raw.at[mine, lanes],
             send_sem=pair_send.at[n], recv_sem=pair_recv.at[n],
             device_id=(sibling, row), device_id_type=MESH,
         )
 
     load_bags = pltpu.make_async_copy(bags_ref, bags, bags_sem)
     load_bags.start()
-    for n in range(chunks):
+    for n in range(yn):
+        local_load(n + yn).start()
         local_load(n).start()
 
     load_bags.wait()
     eighth = bags.shape[0] // 4
     own_ids = pl.ds(pl.multiple_of(row * eighth, 8), eighth)
     ids[own_ids, :] = jnp.concatenate([bags[q * eighth : (q + 1) * eighth, :] for q in range(4)], axis=1)
-    pl.semaphore_wait(barrier, yn * rows - 1 + zn)
+    flat[pl.ds(length, 8), :] = jnp.zeros((8, LANES), jnp.float32)
+
     for n in range(chunks):
-        pair_copy(n).start()
-    flat[pl.ds(length, 8), :] = jnp.zeros((8, LANES), jnp.float32)
+        local_load(n).wait()
 
     def transpose(n):
         c, lanes = chunk_at(n % yn, core if n < yn else 1 - core)
-        local_load(n).wait()
         pair_copy(n).wait_recv()
 
         def step(t, carry):
@@ -129,13 +132,17 @@
         ).start()
         return carry
 
+    pl.semaphore_wait(barrier, yn * rows - 1 + zn)
+    for n in range(chunks):
+        pair_copy(n).start()
+    transpose(0)
     lax.fori_loop(1, rows, send_ids, 0)
-    transpose(0)
-    transpose(1)
     send_blocks(0)
-    transpose(2 % chunks)
-    send_blocks(1)
-    for n in range(3, chunks):
+    for n in range(1, yn):
+        transpose(n)
+        if n > 1:
+            send_blocks(n - 1)
+    for n in range(yn, chunks):
         transpose(n)
 
     others = (rows - 1) * eighth
@@ -176,8 +183,6 @@
             src_ref=part.at[xx], dst_ref=x_in.at[x], send_sem=x_send, recv_sem=x_recv,
             device_id=(col, z * xn + xx), device_id_type=MESH,
         ).start()
-    for n in range(2, yn - 1):
-        send_blocks(n)
     x_rest = part.at[pl.ds(0, xn - 1)]
     pltpu.make_async_copy(x_rest, x_rest, x_recv).wait()
     total = part[x]
@@ -195,8 +200,7 @@
                 src_ref=held.at[zz, kk], dst_ref=z_in.at[z * 2 + core], send_sem=z_send, recv_sem=z_recv,
                 device_id=(y * 2 + kk, zz * xn + x), device_id_type=MESH,
             ).start()
-    if yn > 2:
-        send_blocks(yn - 1)
+    send_blocks(yn - 1)
     own = pltpu.make_async_copy(block(col, row), landing, own_sem)
     own.start()
     z_in[z * 2 + core] = held[z, core]
@@ -231,8 +235,8 @@
     row_table, pooled = pl.pallas_call(
         functools.partial(kernel, zn, xn, span),
         out_shape=[
-            jax.ShapeDtypeStruct((rows, span, half * chunks), f32),
-            jax.ShapeDtypeStruct((bag_rows.shape[0], half), f32),
+            pltpu.VMEM((rows, span, half * chunks), f32),
+            pltpu.VMEM((bag_rows.shape[0], half), f32),
         ],
         in_specs=[pl.BlockSpec(memory_space=pltpu.HBM)] * 2,
         out_specs=[pl.BlockSpec(memory_space=pl.ANY), pl.BlockSpec(memory_space=pltpu.VMEM)],
@@ -251,7 +255,7 @@
             dma((chunks,)), dma((chunks,)), dma((chunks,)),
             dma, dma, dma, dma, dma, dma, dma, dma, dma, dma, dma,
         ],
-        compiler_params=pltpu.CompilerParams(has_side_effects=True, collective_id=0, vmem_limit_bytes=40 * 1024 * 1024),
+        compiler_params=pltpu.CompilerParams(has_side_effects=True, collective_id=0, vmem_limit_bytes=56 * 1024 * 1024),
     )(column_table.T, bag_rows)
     return row_table, pooled
 

time: 73.6 us -> 70.7 us (0.961)
  local copies, waits for them, and re-layouts: 4.23 us -> 1.93 us
    unnamed x6 -> x2, local copies, waits for them, and re-layouts: 4.23 us -> 1.93 us
where the time goes in v3:
time: 70.7 us; the launch traced here: 70.5 us
  Pallas kernels  68 us (96%)
  local copies, waits for them, and re-layouts  1.93 us (3%)
    pallas_call x1, Pallas kernels, per_device(): pl.pallas_call(functools.partial(kernel, zn, xn, span), out_shape=[pltpu....  68 us
    unnamed x2, local copies, waits for them, and re-layouts  1.93 us

profile of v3, /device:TPU:1, one launch (start us, length us, event | category | flops | bytes accessed | tf_op | source)
XLA Modules:
  0.0 70.5 jit_solution(2360483971353161523)
XLA Ops:
  0.6 68.0 %shard_map.41 = (f32[32,32,512]{2,1,0:T(8,128)S(1)}, f32[32,64]{1,0:T(8,128)S(1)}) custom-call(f32[64,8192]{1,0:T(8,128)} %bitcast.1, s32[32,32]{1,0:T(8,128)} %bags_ref.1), custom_call_target="tpu_custom_call" | custom-call | tf_op jit(solution)/shard_map/pallas_call | solution.py:235
  68.6 1.3 %copy.6 = f32[32,32,512]{2,1,0:T(8,128)} copy(f32[32,32,512]{2,1,0:T(8,128)S(1)} %get-tuple-element.2) | data formatting | bytes 4194304
  69.9 0.6 copy.7

commit v4 on v3

v4 whole, which is shorter than its diff:
```python
import functools

import jax
import jax.numpy as jnp
from jax import lax
from jax.experimental import pallas as pl
from jax.experimental.pallas import tpu as pltpu
from jax.sharding import PartitionSpec as P

MESH = pl.DeviceIdType.MESH
LANES = 128
BAG_LEN = 32


def apart(d, n):
    return min(d, n - d)


def kernel(
    zn, xn, span, table_ref, bags_ref, out_ref, pooled_ref,
    raw, flat, bags, ids, near, part2, part, x_in, held, z_in, spot,
    load_sem, pair_send, pair_recv, ids_send, ids_recv, move_send, move_recv,
    x_send, x_recv, z_send, z_recv, spot_sem, own_sem, bags_sem, wave,
):
    rows = zn * xn
    half, length = table_ref.shape
    width = rows * span
    chunks = length // width
    yn = chunks // 2
    col = lax.axis_index("col")
    row = lax.axis_index("row")
    y, core = col // 2, col % 2
    z, x = row // xn, row % xn
    sibling = y * 2 + (1 - core)
    order = sorted(range(yn), key=lambda d: apart(d, yn))

    def load_of_pair(n):
        return n + yn if n < yn else n - yn

    def chunk_at(i, parity):
        c = lax.rem(y + order[i], yn) * 2 + parity
        return c, pl.ds(pl.multiple_of(c * width, LANES), width)

    def local_load(n):
        c, lanes = chunk_at(n % yn, core if n < yn else 1 - core)
        mine = pl.ds(pl.multiple_of(core * half, 8), half)
        return pltpu.make_async_copy(table_ref.at[:, lanes], raw.at[mine, lanes], load_sem.at[n])

    def pair_copy(n):
        c, lanes = chunk_at(n % yn, 1 - core if n < yn else core)
        mine = pl.ds(pl.multiple_of(core * half, 8), half)
        return pltpu.make_async_remote_copy(
            src_ref=raw.at[mine, lanes], dst_ref=raw.at[mine, lanes],
            send_sem=pair_send.at[n], recv_sem=pair_recv.at[n],
            device_id=(sibling, row), device_id_type=MESH,
        )

    load_bags = pltpu.make_async_copy(bags_ref, bags, bags_sem)
    load_bags.start()
    for n in range(yn):
        local_load(n + yn).start()
        local_load(n).start()

    away = sorted(range(1, zn), key=lambda d: -apart(d, zn))
    beside = [(0, d) for d in range(1, xn) if apart(d, xn) == 1] + [(d, 0) for d in range(1, yn) if apart(d, yn) == 1]
    columns = [(dy, dx) for dy in range(yn) for dx in range(xn)]
    rounds = yn // 2 + xn // 2

    def device(dy, dz, dx):
        return lax.rem(y + dy, yn) * 2 + core, lax.rem(z + dz, zn) * xn + lax.rem(x + dx, xn)

    def signal(sem, to):
        pl.semaphore_signal(sem, inc=1, device_id=to, device_id_type=MESH)

    def tell(n):
        for to in [device(0, dz, 0) for dz in away] if n == 1 else [device(dy, 0, dx) for dy, dx in beside]:
            signal(wave.at[n - 1], to)

    def hear(n):
        pl.semaphore_wait(wave.at[n - 1], zn - 1 if n == 1 else len(beside))

    barrier = pltpu.get_barrier_semaphore()
    for dz in away:
        signal(barrier, device(0, dz, 0))
    for dy, dx in beside:
        signal(barrier, device(dy, 0, dx))
    signal(barrier, (sibling, row))

    load_bags.wait()
    eighth = bags.shape[0] // 4
    own_ids = pl.ds(pl.multiple_of((x * zn + z) * eighth, 8), eighth)
    line_ids = pl.ds(pl.multiple_of(x * zn * eighth, 8), zn * eighth)
    ids[own_ids, :] = jnp.concatenate([bags[q * eighth : (q + 1) * eighth, :] for q in range(4)], axis=1)
    flat[pl.ds(length, 8), :] = jnp.zeros((8, LANES), jnp.float32)

    def transpose(n):
        c, lanes = chunk_at(n % yn, core if n < yn else 1 - core)
        pair_copy(n).wait_recv()

        def step(t, carry):
            at = pl.ds(pl.multiple_of(c * width + t * LANES, LANES), LANES)
            flat[at, :] = raw[:, at].T
            return carry

        lax.fori_loop(0, width // LANES, step, 0)

    def block(c, rr):
        return flat.at[pl.ds(pl.multiple_of(c * width + rr * span, 8), span)]

    landing = out_ref.at[row, :, pl.ds(pl.multiple_of(y * LANES, LANES), LANES)]

    def send_blocks(chosen, hops):
        for dz in hops:
            for dy, dx in chosen:
                if (dy, dz, dx) == (0, 0, 0):
                    continue
                c, rr = device(dy, dz, dx)
                pltpu.make_async_remote_copy(
                    src_ref=block(c, rr), dst_ref=landing, send_sem=move_send, recv_sem=move_recv,
                    device_id=(c, rr), device_id_type=MESH,
                ).start()

    def send_ids(which, to, n):
        pltpu.make_async_remote_copy(
            src_ref=ids.at[which], dst_ref=ids.at[which], send_sem=ids_send.at[n], recv_sem=ids_recv.at[n],
            device_id=to, device_id_type=MESH,
        ).start()

    z_ids = ids.at[pl.ds(0, (zn - 1) * eighth)]
    x_ids = ids.at[pl.ds(0, (xn - 1) * zn * eighth)]

    reached = [[c for c in columns if apart(c[0], yn) + apart(c[1], xn) == n] for n in range(rounds + 1)]
    early = [c for c in reached[1] if c[0] == 0]
    late = [c for c in reached[1] if c[0] != 0]
    long_hops, short_hops = away[: (zn - 1) // 2], away[(zn - 1) // 2 :]

    pl.semaphore_wait(barrier, zn + len(beside))
    for dz in away:
        send_ids(own_ids, device(0, dz, 0), 0)
    for n in range(chunks):
        local_load(load_of_pair(n)).wait()
        pair_copy(n).start()
    transpose(0)
    tell(1)
    send_blocks([(0, 0)], long_hops)
    for n in range(1, yn):
        transpose(n)
    hear(1)
    tell(2)
    send_blocks(early, away + [0])
    pltpu.make_async_copy(z_ids, z_ids, ids_recv.at[0]).wait()
    hear(2)
    for dx in range(1, xn):
        send_ids(line_ids, device(0, 0, dx), 1)
    for n in range(2, rounds):
        tell(n + 1)
        send_blocks(reached[n], away + [0])
        hear(n + 1)
    for n in range(yn, chunks):
        transpose(n)

    pltpu.make_async_copy(x_ids, x_ids, ids_recv.at[1]).wait()
    every = ids[...]
    every = jnp.where(every // length == row, every % length, length)
    every = jnp.where(core == 0, every, pltpu.roll(every, LANES // 2, 1))
    folded = rows * eighth // 2
    front = lax.broadcasted_iota(jnp.int32, (folded, LANES), 1) < LANES // 2
    near[...] = jnp.where(front, every[:folded], pltpu.roll(every[folded:], LANES // 2, 1))
    to_scalar = pltpu.make_async_copy(near, spot, spot_sem)
    to_scalar.start()
    to_scalar.wait()

    def gather(t, carry):
        for part_of in range(2):
            for q in range(2):
                sums = [None] * 4
                for l in range(BAG_LEN):
                    at = spot[t, (part_of * 2 + q) * BAG_LEN + l]
                    value = flat[pl.ds(at, 1), :]
                    sums[l % 4] = value if sums[l % 4] is None else sums[l % 4] + value
                part2[q, pl.ds(part_of * folded + t, 1), :] = (sums[0] + sums[1]) + (sums[2] + sums[3])
        return carry

    lax.fori_loop(0, folded, gather, 0)

    low = lax.broadcasted_iota(jnp.int32, (8, LANES), 1) < half

    def split(s, carry):
        at = pl.ds(pl.multiple_of(s * 8, 8), 8)
        first, second = part2[0, at, :], part2[1, at, :]
        part[s // zn, s % zn, 0] = jnp.where(low, first, pltpu.roll(second, half, 1))
        part[s // zn, s % zn, 1] = jnp.where(low, pltpu.roll(first, half, 1), second)
        return carry

    lax.fori_loop(0, rows, split, 0)

    for d in range(1, xn):
        xx = lax.rem(x + d, xn)
        pltpu.make_async_remote_copy(
            src_ref=part.at[xx], dst_ref=x_in.at[x], send_sem=x_send, recv_sem=x_recv,
            device_id=(col, z * xn + xx), device_id_type=MESH,
        ).start()
    x_rest = part.at[pl.ds(0, xn - 1)]
    pltpu.make_async_copy(x_rest, x_rest, x_recv).wait()
    total = part[x]
    for d in range(1, xn):
        total = total + x_in[lax.rem(x + d, xn)]
    held[...] = total

    for d in range(zn):
        zz = lax.rem(z + d, zn)
        for e in range(2):
            if d == 0 and e == 0:
                continue
            kk = core if e == 0 else 1 - core
            pltpu.make_async_remote_copy(
                src_ref=held.at[zz, kk], dst_ref=z_in.at[z * 2 + core], send_sem=z_send, recv_sem=z_recv,
                device_id=(y * 2 + kk, zz * xn + x), device_id_type=MESH,
            ).start()
    send_blocks(reached[rounds], away + [0])
    send_blocks(late, away + [0])
    send_blocks([(0, 0)], short_hops)
    own = pltpu.make_async_copy(block(col, row), landing, own_sem)
    own.start()
    z_in[z * 2 + core] = held[z, core]
    z_rest = z_in.at[pl.ds(0, 2 * zn - 1)]
    pltpu.make_async_copy(z_rest, z_rest, z_recv).wait()
    for k in range(2):
        total = z_in[k]
        for d in range(1, zn):
            total = total + z_in[d * 2 + k]
        pooled_ref[pl.ds(k * 16, 8), :] = total[:, :half]
        pooled_ref[pl.ds(k * 16 + 8, 8), :] = pltpu.roll(total, half, 1)[:, :half]

    own.wait()
    moved = flat.at[pl.ds(0, (yn * rows - 1) * span)]
    pltpu.make_async_copy(moved, moved, move_recv).wait()
    pltpu.make_async_copy(moved, moved, move_send).wait()
    pltpu.make_async_copy(z_ids, z_ids, ids_send.at[0]).wait()
    pltpu.make_async_copy(x_ids, x_ids, ids_send.at[1]).wait()
    pltpu.make_async_copy(x_rest, x_rest, x_send).wait()
    pltpu.make_async_copy(z_rest, z_rest, z_send).wait()
    for n in range(chunks):
        pair_copy(n).wait_send()


def write_out(table_ref, pooled_ref, table_out, pooled_out, sems):
    table = pltpu.make_async_copy(table_ref, table_out, sems.at[0])
    pooled = pltpu.make_async_copy(pooled_ref, pooled_out, sems.at[1])
    table.start()
    pooled.start()
    table.wait()
    pooled.wait()


def per_device(zn, xn, column_table, bag_rows):
    rows = zn * xn
    chunks = lax.axis_size("col")
    length, half = column_table.shape
    span = length // (rows * chunks)
    f32 = jnp.float32
    dma = pltpu.SemaphoreType.DMA
    row_table, pooled = pl.pallas_call(
        functools.partial(kernel, zn, xn, span),
        out_shape=[
            pltpu.VMEM((rows, span, half * chunks), f32),
            pltpu.VMEM((bag_rows.shape[0], half), f32),
        ],
        in_specs=[pl.BlockSpec(memory_space=pltpu.HBM)] * 2,
        out_specs=[pl.BlockSpec(memory_space=pl.ANY), pl.BlockSpec(memory_space=pltpu.VMEM)],
        scratch_shapes=[
            pltpu.VMEM((2 * half, length), f32),
            pltpu.VMEM((length + 8, LANES), f32),
            pltpu.VMEM(bag_rows.shape, jnp.int32),
            pltpu.VMEM((rows * 8, LANES), jnp.int32),
            pltpu.VMEM((rows * 4, LANES), jnp.int32),
            pltpu.VMEM((2, rows * 8, LANES), f32),
            pltpu.VMEM((xn, zn, 2, 8, LANES), f32),
            pltpu.VMEM((xn, zn, 2, 8, LANES), f32),
            pltpu.VMEM((zn, 2, 8, LANES), f32),
            pltpu.VMEM((zn * 2, 8, LANES), f32),
            pltpu.SMEM((rows * 4, LANES), jnp.int32),
            dma((chunks,)), dma((chunks,)), dma((chunks,)),
            dma((2,)), dma((2,)), dma, dma, dma, dma, dma, dma, dma, dma, dma,
            pltpu.SemaphoreType.REGULAR((chunks // 4 + xn // 2,)),
        ],
        compiler_params=pltpu.CompilerParams(has_side_effects=True, collective_id=0, vmem_limit_bytes=56 * 1024 * 1024),
    )(column_table.T, bag_rows)
    return pl.pallas_call(
        write_out,
        out_shape=[
            jax.ShapeDtypeStruct(row_table.shape, f32),
            jax.ShapeDtypeStruct(pooled.shape, f32),
        ],
        in_specs=[pl.BlockSpec(memory_space=pl.ANY)] * 2,
        out_specs=[pl.BlockSpec(memory_space=pl.ANY)] * 2,
        scratch_shapes=[dma((2,))],
        compiler_params=pltpu.CompilerParams(vmem_limit_bytes=16 * 1024 * 1024),
    )(row_table, pooled)


def solution(mesh):
    rows = mesh.shape["row"]
    xn = 4 if rows == 32 else 2
    return jax.shard_map(
        functools.partial(per_device, rows // xn, xn),
        mesh=mesh,
        in_specs=(P("row", "col"), P("row", None)),
        out_specs=(P(None, ("col", "row"), None), P("row", "col")),
        check_vma=False,
    )
```

time: 70.7 us -> 67.7 us (0.958)
  the two profiles are of different devices: /device:TPU:1 before, /device:TPU:7 now
where the time goes in v4:
time: 67.7 us; the launch traced here: 67.5 us
  Pallas kernels  66.8 us (99%)
    pallas_call x1, Pallas kernels, per_device(): pl.pallas_call(functools.partial(kernel, zn, xn, span), out_shape=[pltpu....  65.5 us

profile of v4, /device:TPU:7, one launch (start us, length us, event | category | flops | bytes accessed | tf_op | source)
XLA Modules:
  0.0 67.5 jit_solution(2312934452917298117)
XLA Ops:
  0.6 65.5 %shard_map.41 = (f32[32,32,512]{2,1,0:T(8,128)S(1)}, f32[32,64]{1,0:T(8,128)S(1)}) custom-call(f32[64,8192]{1,0:T(8,128)} %bitcast.1, s32[32,32]{1,0:T(8,128)} %bags_ref.1), custom_call_target="tpu_custom_call" | custom-call | tf_op jit(solution)/shard_map/pallas_call | solution.py:263
  66.1 1.3 %shard_map.42 = (f32[32,32,512]{2,1,0:T(8,128)}, f32[32,64]{1,0:T(8,128)}) custom-call(f32[32,32,512]{2,1,0:T(8,128)S(1)} %get-tuple-element.4.table_ref, f32[32,64]{1,0:T(8,128)S(1)} %get-tuple-element.5.pooled_ref), custom_call_target="tpu_custom_call" | custom-call | tf_op jit(solution)/shard_map/pallas_call | solution.py:289

commit v5 on v4

--- a/solution.py
+++ b/solution.py
@@ -159,6 +159,8 @@
     for n in range(yn, chunks):
         transpose(n)
 
+    send_blocks(reached[rounds], away + [0])
+    send_blocks(late, away + [0])
     pltpu.make_async_copy(x_ids, x_ids, ids_recv.at[1]).wait()
     every = ids[...]
     every = jnp.where(every // length == row, every % length, length)
@@ -217,8 +219,6 @@
                 src_ref=held.at[zz, kk], dst_ref=z_in.at[z * 2 + core], send_sem=z_send, recv_sem=z_recv,
                 device_id=(y * 2 + kk, zz * xn + x), device_id_type=MESH,
             ).start()
-    send_blocks(reached[rounds], away + [0])
-    send_blocks(late, away + [0])
     send_blocks([(0, 0)], short_hops)
     own = pltpu.make_async_copy(block(col, row), landing, own_sem)
     own.start()

time: 67.7 us -> 63.6 us (0.939)
  the two profiles are of different devices: /device:TPU:7 before, /device:TPU:1 now
where the time goes in v5:
time: 63.6 us; the launch traced here: 63.4 us
  Pallas kernels  62.8 us (99%)
  between operations  0.64 us (1%)
    pallas_call x1, Pallas kernels, per_device(): pl.pallas_call(functools.partial(kernel, zn, xn, span), out_shape=[pltpu....  61.4 us
    pallas_call x1, Pallas kernels, per_device(): pl.pallas_call(write_out, out_shape=[jax.ShapeDtypeStruct(row_table.shape...  1.34 us

profile of v5, /device:TPU:1, one launch (start us, length us, event | category | flops | bytes accessed | tf_op | source)
XLA Modules:
  0.0 63.4 jit_solution(8371423258627843811)
XLA Ops:
  0.6 61.4 %shard_map.41 = (f32[32,32,512]{2,1,0:T(8,128)S(1)}, f32[32,64]{1,0:T(8,128)S(1)}) custom-call(f32[64,8192]{1,0:T(8,128)} %bitcast.1, s32[32,32]{1,0:T(8,128)} %bags_ref.1), custom_call_target="tpu_custom_call" | custom-call | tf_op jit(solution)/shard_map/pallas_call | solution.py:263
  62.1 1.3 %shard_map.42 = (f32[32,32,512]{2,1,0:T(8,128)}, f32[32,64]{1,0:T(8,128)}) custom-call(f32[32,32,512]{2,1,0:T(8,128)S(1)} %get-tuple-element.4.table_ref, f32[32,64]{1,0:T(8,128)S(1)} %get-tuple-element.5.pooled_ref), custom_call_target="tpu_custom_call" | custom-call | tf_op jit(solution)/shard_map/pallas_call | solution.py:289

commit v6 on v5

--- a/solution.py
+++ b/solution.py
@@ -14,6 +14,14 @@
 
 def apart(d, n):
     return min(d, n - d)
+
+
+def mate(v, m, n):
+    if m == 0:
+        return v
+    if m == n - 1:
+        return n - 1 - v
+    return v + 1 - 2 * lax.rem(v, 2) if m == 1 else lax.rem(v + 2, n)
 
 
 def kernel(
@@ -32,13 +40,13 @@
     y, core = col // 2, col % 2
     z, x = row // xn, row % xn
     sibling = y * 2 + (1 - core)
-    order = sorted(range(yn), key=lambda d: apart(d, yn))
+    order = sorted(range(yn), key=lambda m: (m > 0, m != yn - 1, m))
 
     def load_of_pair(n):
         return n + yn if n < yn else n - yn
 
     def chunk_at(i, parity):
-        c = lax.rem(y + order[i], yn) * 2 + parity
+        c = mate(y, order[i], yn) * 2 + parity
         return c, pl.ds(pl.multiple_of(c * width, LANES), width)
 
     def local_load(n):
@@ -111,10 +119,11 @@
 
     def send_blocks(chosen, hops):
         for dz in hops:
-            for dy, dx in chosen:
-                if (dy, dz, dx) == (0, 0, 0):
+            for my, mx in chosen:
+                if (my, dz, mx) == (0, 0, 0):
                     continue
-                c, rr = device(dy, dz, dx)
+                c = mate(y, my, yn) * 2 + core
+                rr = lax.rem(z + dz, zn) * xn + mate(x, mx, xn)
                 pltpu.make_async_remote_copy(
                     src_ref=block(c, rr), dst_ref=landing, send_sem=move_send, recv_sem=move_recv,
                     device_id=(c, rr), device_id_type=MESH,
@@ -129,79 +138,91 @@
     z_ids = ids.at[pl.ds(0, (zn - 1) * eighth)]
     x_ids = ids.at[pl.ds(0, (xn - 1) * zn * eighth)]
 
-    reached = [[c for c in columns if apart(c[0], yn) + apart(c[1], xn) == n] for n in range(rounds + 1)]
-    early = [c for c in reached[1] if c[0] == 0]
-    late = [c for c in reached[1] if c[0] != 0]
+    def hops_to(my, mx):
+        return (2 if my == 2 else min(my, 1)) + (2 if mx == 2 else min(mx, 1))
+
+    quad = [c for c in columns if max(c) < 2]
+    last = [c for c in quad if hops_to(*c) == 1]
+    reached = [[c for c in columns if c not in quad and hops_to(*c) == n] for n in range(rounds + 1)]
+    reached[rounds] += [c for c in quad if hops_to(*c) == 2]
     long_hops, short_hops = away[: (zn - 1) // 2], away[(zn - 1) // 2 :]
 
     pl.semaphore_wait(barrier, zn + len(beside))
-    for dz in away:
-        send_ids(own_ids, device(0, dz, 0), 0)
+    tell(1)
     for n in range(chunks):
         local_load(load_of_pair(n)).wait()
         pair_copy(n).start()
     transpose(0)
-    tell(1)
+    for dz in away:
+        send_ids(own_ids, device(0, dz, 0), 0)
     send_blocks([(0, 0)], long_hops)
     for n in range(1, yn):
         transpose(n)
     hear(1)
     tell(2)
-    send_blocks(early, away + [0])
+    send_blocks(reached[1], away + [0])
     pltpu.make_async_copy(z_ids, z_ids, ids_recv.at[0]).wait()
     hear(2)
     for dx in range(1, xn):
         send_ids(line_ids, device(0, 0, dx), 1)
-    for n in range(2, rounds):
-        tell(n + 1)
-        send_blocks(reached[n], away + [0])
-        hear(n + 1)
+    if rounds > 2:
+        tell(3)
+        send_blocks(reached[2], away + [0])
     for n in range(yn, chunks):
         transpose(n)
 
-    send_blocks(reached[rounds], away + [0])
-    send_blocks(late, away + [0])
     pltpu.make_async_copy(x_ids, x_ids, ids_recv.at[1]).wait()
     every = ids[...]
     every = jnp.where(every // length == row, every % length, length)
     every = jnp.where(core == 0, every, pltpu.roll(every, LANES // 2, 1))
-    folded = rows * eighth // 2
-    front = lax.broadcasted_iota(jnp.int32, (folded, LANES), 1) < LANES // 2
-    near[...] = jnp.where(front, every[:folded], pltpu.roll(every[folded:], LANES // 2, 1))
+    fold = zn * eighth // 2
+    front = lax.broadcasted_iota(jnp.int32, (fold, LANES), 1) < LANES // 2
+    for d in range(xn):
+        upper, lower = every[d * 2 * fold : (d * 2 + 1) * fold], every[(d * 2 + 1) * fold : (d * 2 + 2) * fold]
+        near[d * fold : (d + 1) * fold, :] = jnp.where(front, upper, pltpu.roll(lower, LANES // 2, 1))
     to_scalar = pltpu.make_async_copy(near, spot, spot_sem)
     to_scalar.start()
     to_scalar.wait()
 
-    def gather(t, carry):
-        for part_of in range(2):
-            for q in range(2):
-                sums = [None] * 4
-                for l in range(BAG_LEN):
-                    at = spot[t, (part_of * 2 + q) * BAG_LEN + l]
-                    value = flat[pl.ds(at, 1), :]
-                    sums[l % 4] = value if sums[l % 4] is None else sums[l % 4] + value
-                part2[q, pl.ds(part_of * folded + t, 1), :] = (sums[0] + sums[1]) + (sums[2] + sums[3])
-        return carry
-
-    lax.fori_loop(0, folded, gather, 0)
-
     low = lax.broadcasted_iota(jnp.int32, (8, LANES), 1) < half
 
-    def split(s, carry):
-        at = pl.ds(pl.multiple_of(s * 8, 8), 8)
-        first, second = part2[0, at, :], part2[1, at, :]
-        part[s // zn, s % zn, 0] = jnp.where(low, first, pltpu.roll(second, half, 1))
-        part[s // zn, s % zn, 1] = jnp.where(low, pltpu.roll(first, half, 1), second)
-        return carry
-
-    lax.fori_loop(0, rows, split, 0)
-
-    for d in range(1, xn):
+    def pool(xx):
+        def gather(t, carry):
+            for h in range(2):
+                for q in range(2):
+                    sums = [None] * 4
+                    for l in range(BAG_LEN):
+                        at = spot[xx * fold + t, (h * 2 + q) * BAG_LEN + l]
+                        value = flat[pl.ds(at, 1), :]
+                        sums[l % 4] = value if sums[l % 4] is None else sums[l % 4] + value
+                    part2[q, pl.ds(h * fold + t, 1), :] = (sums[0] + sums[1]) + (sums[2] + sums[3])
+            return carry
+
+        lax.fori_loop(0, fold, gather, 0)
+
+        for s in range(zn):
+            first, second = part2[0, s * 8 : s * 8 + 8, :], part2[1, s * 8 : s * 8 + 8, :]
+            part[xx, s, 0] = jnp.where(low, first, pltpu.roll(second, half, 1))
+            part[xx, s, 1] = jnp.where(low, pltpu.roll(first, half, 1), second)
+
+    def send_part(d):
         xx = lax.rem(x + d, xn)
         pltpu.make_async_remote_copy(
             src_ref=part.at[xx], dst_ref=x_in.at[x], send_sem=x_send, recv_sem=x_recv,
             device_id=(col, z * xn + xx), device_id_type=MESH,
         ).start()
+
+    for d in range(1, xn):
+        pool(lax.rem(x + d, xn))
+        n = d + 2
+        if n <= rounds:
+            hear(n)
+            if n < rounds:
+                tell(n + 1)
+                send_blocks(reached[n], away + [0])
+        send_part(d)
+    send_blocks(reached[rounds], away + [0])
+    pool(x)
     x_rest = part.at[pl.ds(0, xn - 1)]
     pltpu.make_async_copy(x_rest, x_rest, x_recv).wait()
     total = part[x]
@@ -219,6 +240,7 @@
                 src_ref=held.at[zz, kk], dst_ref=z_in.at[z * 2 + core], send_sem=z_send, recv_sem=z_recv,
                 device_id=(y * 2 + kk, zz * xn + x), device_id_type=MESH,
             ).start()
+    send_blocks(last, away + [0])
     send_blocks([(0, 0)], short_hops)
     own = pltpu.make_async_copy(block(col, row), landing, own_sem)
     own.start()
@@ -274,7 +296,7 @@
             pltpu.VMEM(bag_rows.shape, jnp.int32),
             pltpu.VMEM((rows * 8, LANES), jnp.int32),
             pltpu.VMEM((rows * 4, LANES), jnp.int32),
-            pltpu.VMEM((2, rows * 8, LANES), f32),
+            pltpu.VMEM((2, zn * 8, LANES), f32),
             pltpu.VMEM((xn, zn, 2, 8, LANES), f32),
             pltpu.VMEM((xn, zn, 2, 8, LANES), f32),
             pltpu.VMEM((zn, 2, 8, LANES), f32),

time: 63.6 us -> 63.2 us (level)
  no operation moved by 1% of the time
where the time goes in v6:
time: 63.2 us; the launch traced here: 63 us
  Pallas kernels  62.4 us (99%)
  between operations  0.64 us (1%)
    pallas_call x1, Pallas kernels, per_device(): pl.pallas_call(functools.partial(kernel, zn, xn, span), out_shape=[pltpu....  61 us
    pallas_call x1, Pallas kernels, per_device(): pl.pallas_call(write_out, out_shape=[jax.ShapeDtypeStruct(row_table.shape...  1.34 us

profile of v6, /device:TPU:1, one launch (start us, length us, event | category | flops | bytes accessed | tf_op | source)
XLA Modules:
  0.0 63.0 jit_solution(10497086260800220780)
XLA Ops:
  0.6 61.0 %shard_map.41 = (f32[32,32,512]{2,1,0:T(8,128)S(1)}, f32[32,64]{1,0:T(8,128)S(1)}) custom-call(f32[64,8192]{1,0:T(8,128)} %bitcast.1, s32[32,32]{1,0:T(8,128)} %bags_ref.1), custom_call_target="tpu_custom_call" | custom-call | tf_op jit(solution)/shard_map/pallas_call | solution.py:285
  61.7 1.3 %shard_map.42 = (f32[32,32,512]{2,1,0:T(8,128)}, f32[32,64]{1,0:T(8,128)}) custom-call(f32[32,32,512]{2,1,0:T(8,128)S(1)} %get-tuple-element.4.table_ref, f32[32,64]{1,0:T(8,128)S(1)} %get-tuple-element.5.pooled_ref), custom_call_target="tpu_custom_call" | custom-call | tf_op jit(solution)/shard_map/pallas_call | solution.py:311

commit v7 on v6

--- a/solution.py
+++ b/solution.py
@@ -63,7 +63,9 @@
             device_id=(sibling, row), device_id_type=MESH,
         )
 
-    load_bags = pltpu.make_async_copy(bags_ref, bags, bags_sem)
+    core_bags = bags.shape[0]
+    own_bags = pl.ds(pl.multiple_of(core * core_bags, 8), core_bags)
+    load_bags = pltpu.make_async_copy(bags_ref.at[own_bags], bags, bags_sem)
     load_bags.start()
     for n in range(yn):
         local_load(n + yn).start()
@@ -95,10 +97,7 @@
     signal(barrier, (sibling, row))
 
     load_bags.wait()
-    eighth = bags.shape[0] // 4
-    own_ids = pl.ds(pl.multiple_of((x * zn + z) * eighth, 8), eighth)
-    line_ids = pl.ds(pl.multiple_of(x * zn * eighth, 8), zn * eighth)
-    ids[own_ids, :] = jnp.concatenate([bags[q * eighth : (q + 1) * eighth, :] for q in range(4)], axis=1)
+    ids[x, z] = jnp.concatenate([bags[g * 4 : (g + 1) * 4, :] for g in range(core_bags // 4)], axis=1)
     flat[pl.ds(length, 8), :] = jnp.zeros((8, LANES), jnp.float32)
 
     def transpose(n):
@@ -129,14 +128,35 @@
                     device_id=(c, rr), device_id_type=MESH,
                 ).start()
 
-    def send_ids(which, to, n):
+    def send_last(chosen):
+        for zz in range(zn):
+            for my, mx in chosen:
+                c = mate(y, my, yn) * 2 + core
+                rr = zz * xn + mate(x, mx, xn)
+
+                def send():
+                    pltpu.make_async_remote_copy(
+                        src_ref=block(c, rr), dst_ref=landing, send_sem=move_send, recv_sem=move_recv,
+                        device_id=(c, rr), device_id_type=MESH,
+                    ).start()
+
+                if (my, mx) != (0, 0):
+                    send()
+                else:
+                    dz = lax.rem(zz - z + zn, zn)
+                    near_z = dz == short_hops[0]
+                    for d in short_hops[1:]:
+                        near_z = near_z | (dz == d)
+                    pl.when(near_z)(send)
+
+    def send_ids(held_ids, to, n):
         pltpu.make_async_remote_copy(
-            src_ref=ids.at[which], dst_ref=ids.at[which], send_sem=ids_send.at[n], recv_sem=ids_recv.at[n],
+            src_ref=held_ids, dst_ref=held_ids, send_sem=ids_send.at[n], recv_sem=ids_recv.at[n],
             device_id=to, device_id_type=MESH,
         ).start()
 
-    z_ids = ids.at[pl.ds(0, (zn - 1) * eighth)]
-    x_ids = ids.at[pl.ds(0, (xn - 1) * zn * eighth)]
+    z_ids = ids.at[0, pl.ds(0, zn - 1)]
+    x_ids = ids.at[pl.ds(0, xn - 1)]
 
     def hops_to(my, mx):
         return (2 if my == 2 else min(my, 1)) + (2 if mx == 2 else min(mx, 1))
@@ -154,7 +174,7 @@
         pair_copy(n).start()
     transpose(0)
     for dz in away:
-        send_ids(own_ids, device(0, dz, 0), 0)
+        send_ids(ids.at[x, z], device(0, dz, 0), 0)
     send_blocks([(0, 0)], long_hops)
     for n in range(1, yn):
         transpose(n)
@@ -164,7 +184,7 @@
     pltpu.make_async_copy(z_ids, z_ids, ids_recv.at[0]).wait()
     hear(2)
     for dx in range(1, xn):
-        send_ids(line_ids, device(0, 0, dx), 1)
+        send_ids(ids.at[x], device(0, 0, dx), 1)
     if rounds > 2:
         tell(3)
         send_blocks(reached[2], away + [0])
@@ -174,12 +194,7 @@
     pltpu.make_async_copy(x_ids, x_ids, ids_recv.at[1]).wait()
     every = ids[...]
     every = jnp.where(every // length == row, every % length, length)
-    every = jnp.where(core == 0, every, pltpu.roll(every, LANES // 2, 1))
-    fold = zn * eighth // 2
-    front = lax.broadcasted_iota(jnp.int32, (fold, LANES), 1) < LANES // 2
-    for d in range(xn):
-        upper, lower = every[d * 2 * fold : (d * 2 + 1) * fold], every[(d * 2 + 1) * fold : (d * 2 + 2) * fold]
-        near[d * fold : (d + 1) * fold, :] = jnp.where(front, upper, pltpu.roll(lower, LANES // 2, 1))
+    near[...] = every
     to_scalar = pltpu.make_async_copy(near, spot, spot_sem)
     to_scalar.start()
     to_scalar.wait()
@@ -188,17 +203,17 @@
 
     def pool(xx):
         def gather(t, carry):
-            for h in range(2):
-                for q in range(2):
-                    sums = [None] * 4
-                    for l in range(BAG_LEN):
-                        at = spot[xx * fold + t, (h * 2 + q) * BAG_LEN + l]
-                        value = flat[pl.ds(at, 1), :]
-                        sums[l % 4] = value if sums[l % 4] is None else sums[l % 4] + value
-                    part2[q, pl.ds(h * fold + t, 1), :] = (sums[0] + sums[1]) + (sums[2] + sums[3])
+            owner, line = t // 4, t % 4
+            for g in range(core_bags // 4):
+                sums = [None] * 4
+                for l in range(BAG_LEN):
+                    at = spot[xx, owner, line, g * BAG_LEN + l]
+                    value = flat[pl.ds(at, 1), :]
+                    sums[l % 4] = value if sums[l % 4] is None else sums[l % 4] + value
+                part2[g // 2, pl.ds(owner * 8 + (g % 2) * 4 + line, 1), :] = (sums[0] + sums[1]) + (sums[2] + sums[3])
             return carry
 
-        lax.fori_loop(0, fold, gather, 0)
+        lax.fori_loop(0, zn * 4, gather, 0)
 
         for s in range(zn):
             first, second = part2[0, s * 8 : s * 8 + 8, :], part2[1, s * 8 : s * 8 + 8, :]
@@ -240,8 +255,7 @@
                 src_ref=held.at[zz, kk], dst_ref=z_in.at[z * 2 + core], send_sem=z_send, recv_sem=z_recv,
                 device_id=(y * 2 + kk, zz * xn + x), device_id_type=MESH,
             ).start()
-    send_blocks(last, away + [0])
-    send_blocks([(0, 0)], short_hops)
+    send_last(last + [(0, 0)])
     own = pltpu.make_async_copy(block(col, row), landing, own_sem)
     own.start()
     z_in[z * 2 + core] = held[z, core]
@@ -293,15 +307,15 @@
         scratch_shapes=[
             pltpu.VMEM((2 * half, length), f32),
             pltpu.VMEM((length + 8, LANES), f32),
-            pltpu.VMEM(bag_rows.shape, jnp.int32),
-            pltpu.VMEM((rows * 8, LANES), jnp.int32),
-            pltpu.VMEM((rows * 4, LANES), jnp.int32),
+            pltpu.VMEM((bag_rows.shape[0] // 2, BAG_LEN), jnp.int32),
+            pltpu.VMEM((xn, zn, 4, LANES), jnp.int32),
+            pltpu.VMEM((xn, zn, 4, LANES), jnp.int32),
             pltpu.VMEM((2, zn * 8, LANES), f32),
             pltpu.VMEM((xn, zn, 2, 8, LANES), f32),
             pltpu.VMEM((xn, zn, 2, 8, LANES), f32),
             pltpu.VMEM((zn, 2, 8, LANES), f32),
             pltpu.VMEM((zn * 2, 8, LANES), f32),
-            pltpu.SMEM((rows * 4, LANES), jnp.int32),
+            pltpu.SMEM((xn, zn, 4, LANES), jnp.int32),
             dma((chunks,)), dma((chunks,)), dma((chunks,)),
             dma((2,)), dma((2,)), dma, dma, dma, dma, dma, dma, dma, dma, dma,
             pltpu.SemaphoreType.REGULAR((chunks // 4 + xn // 2,)),

time: 63.2 us -> 61.6 us (0.975)
  Pallas kernels: 62.4 us -> 60.3 us
    pallas_call x1, Pallas kernels: 61 us -> 58.9 us  [per_device(): pl.pallas_call(functools.partial(kernel, zn, xn, span), out_shape=[pltpu....]
where the time goes in v7:
time: 61.6 us; the launch traced here: 60.9 us
  Pallas kernels  60.3 us (98%)
  between operations  0.64 us (1%)
    pallas_call x1, Pallas kernels, per_device(): pl.pallas_call(functools.partial(kernel, zn, xn, span), out_shape=[pltpu....  58.9 us
    pallas_call x1, Pallas kernels, per_device(): pl.pallas_call(write_out, out_shape=[jax.ShapeDtypeStruct(row_table.shape...  1.34 us

profile of v7, /device:TPU:1, one launch (start us, length us, event | category | flops | bytes accessed | tf_op | source)
XLA Modules:
  0.0 60.9 jit_solution(13593727899114744373)
XLA Ops:
  0.6 58.9 %shard_map.41 = (f32[32,32,512]{2,1,0:T(8,128)S(1)}, f32[32,64]{1,0:T(8,128)S(1)}) custom-call(f32[64,8192]{1,0:T(8,128)} %bitcast.1, s32[32,32]{1,0:T(8,128)} %bags_ref.1), custom_call_target="tpu_custom_call" | custom-call | tf_op jit(solution)/shard_map/pallas_call | solution.py:299
  59.6 1.3 %shard_map.42 = (f32[32,32,512]{2,1,0:T(8,128)}, f32[32,64]{1,0:T(8,128)}) custom-call(f32[32,32,512]{2,1,0:T(8,128)S(1)} %get-tuple-element.4.table_ref, f32[32,64]{1,0:T(8,128)S(1)} %get-tuple-element.5.pooled_ref), custom_call_target="tpu_custom_call" | custom-call | tf_op jit(solution)/shard_map/pallas_call | solution.py:325

commit v8 on v7

--- a/solution.py
+++ b/solution.py
@@ -66,9 +66,10 @@
     core_bags = bags.shape[0]
     own_bags = pl.ds(pl.multiple_of(core * core_bags, 8), core_bags)
     load_bags = pltpu.make_async_copy(bags_ref.at[own_bags], bags, bags_sem)
+    for n in range(yn):
+        local_load(load_of_pair(n)).start()
     load_bags.start()
     for n in range(yn):
-        local_load(n + yn).start()
         local_load(n).start()
 
     away = sorted(range(1, zn), key=lambda d: -apart(d, zn))
@@ -83,11 +84,11 @@
         pl.semaphore_signal(sem, inc=1, device_id=to, device_id_type=MESH)
 
     def tell(n):
-        for to in [device(0, dz, 0) for dz in away] if n == 1 else [device(dy, 0, dx) for dy, dx in beside]:
-            signal(wave.at[n - 1], to)
+        for dy, dx in beside:
+            signal(wave.at[n - 1], device(dy, 0, dx))
 
     def hear(n):
-        pl.semaphore_wait(wave.at[n - 1], zn - 1 if n == 1 else len(beside))
+        pl.semaphore_wait(wave.at[n - 1], len(beside))
 
     barrier = pltpu.get_barrier_semaphore()
     for dz in away:
@@ -176,11 +177,12 @@
     for dz in away:
         send_ids(ids.at[x, z], device(0, dz, 0), 0)
     send_blocks([(0, 0)], long_hops)
-    for n in range(1, yn):
-        transpose(n)
+    transpose(1)
     hear(1)
     tell(2)
     send_blocks(reached[1], away + [0])
+    for n in range(2, yn):
+        transpose(n)
     pltpu.make_async_copy(z_ids, z_ids, ids_recv.at[0]).wait()
     hear(2)
     for dx in range(1, xn):

time: 61.6 us -> 61.4 us (level)
  no operation moved by 1% of the time
where the time goes in v8:
time: 61.4 us; the launch traced here: 60.6 us
  Pallas kernels  60 us (98%)
  between operations  0.64 us (1%)
    pallas_call x1, Pallas kernels, per_device(): pl.pallas_call(functools.partial(kernel, zn, xn, span), out_shape=[pltpu....  58.7 us
    pallas_call x1, Pallas kernels, per_device(): pl.pallas_call(write_out, out_shape=[jax.ShapeDtypeStruct(row_table.shape...  1.34 us

profile of v8, /device:TPU:1, one launch (start us, length us, event | category | flops | bytes accessed | tf_op | source)
XLA Modules:
  0.0 60.6 jit_solution(16519459235537478882)
XLA Ops:
  0.6 58.7 %shard_map.41 = (f32[32,32,512]{2,1,0:T(8,128)S(1)}, f32[32,64]{1,0:T(8,128)S(1)}) custom-call(f32[64,8192]{1,0:T(8,128)} %bitcast.1, s32[32,32]{1,0:T(8,128)} %bags_ref.1), custom_call_target="tpu_custom_call" | custom-call | tf_op jit(solution)/shard_map/pallas_call | solution.py:301
  59.3 1.3 %shard_map.42 = (f32[32,32,512]{2,1,0:T(8,128)}, f32[32,64]{1,0:T(8,128)}) custom-call(f32[32,32,512]{2,1,0:T(8,128)S(1)} %get-tuple-element.4.table_ref, f32[32,64]{1,0:T(8,128)S(1)} %get-tuple-element.5.pooled_ref), custom_call_target="tpu_custom_call" | custom-call | tf_op jit(solution)/shard_map/pallas_call | solution.py:327

commit v9 on v8

--- a/solution.py
+++ b/solution.py
@@ -45,21 +45,33 @@
     def load_of_pair(n):
         return n + yn if n < yn else n - yn
 
+    split = 4 if width % (4 * LANES) == 0 else 1
+
+    def pieces(n):
+        return split if n == 0 else 1
+
+    def slot(n, p):
+        return n if p == 0 else chunks + p - 1
+
     def chunk_at(i, parity):
-        c = mate(y, order[i], yn) * 2 + parity
-        return c, pl.ds(pl.multiple_of(c * width, LANES), width)
+        return mate(y, order[i], yn) * 2 + parity
+
+    def lanes_of(c, p, parts):
+        return pl.ds(pl.multiple_of(c * width + p * (width // parts), LANES), width // parts)
 
     def local_load(n):
-        c, lanes = chunk_at(n % yn, core if n < yn else 1 - core)
+        c = chunk_at(n % yn, core if n < yn else 1 - core)
+        lanes = lanes_of(c, 0, 1)
         mine = pl.ds(pl.multiple_of(core * half, 8), half)
         return pltpu.make_async_copy(table_ref.at[:, lanes], raw.at[mine, lanes], load_sem.at[n])
 
-    def pair_copy(n):
-        c, lanes = chunk_at(n % yn, 1 - core if n < yn else core)
+    def pair_copy(n, p):
+        c = chunk_at(n % yn, 1 - core if n < yn else core)
+        lanes = lanes_of(c, p, pieces(n))
         mine = pl.ds(pl.multiple_of(core * half, 8), half)
         return pltpu.make_async_remote_copy(
             src_ref=raw.at[mine, lanes], dst_ref=raw.at[mine, lanes],
-            send_sem=pair_send.at[n], recv_sem=pair_recv.at[n],
+            send_sem=pair_send.at[slot(n, p)], recv_sem=pair_recv.at[slot(n, p)],
             device_id=(sibling, row), device_id_type=MESH,
         )
 
@@ -102,15 +114,17 @@
     flat[pl.ds(length, 8), :] = jnp.zeros((8, LANES), jnp.float32)
 
     def transpose(n):
-        c, lanes = chunk_at(n % yn, core if n < yn else 1 - core)
-        pair_copy(n).wait_recv()
+        c = chunk_at(n % yn, core if n < yn else 1 - core)
+        blocks = width // LANES // pieces(n)
 
         def step(t, carry):
             at = pl.ds(pl.multiple_of(c * width + t * LANES, LANES), LANES)
             flat[at, :] = raw[:, at].T
             return carry
 
-        lax.fori_loop(0, width // LANES, step, 0)
+        for p in range(pieces(n)):
+            pair_copy(n, p).wait_recv()
+            lax.fori_loop(p * blocks, (p + 1) * blocks, step, 0)
 
     def block(c, rr):
         return flat.at[pl.ds(pl.multiple_of(c * width + rr * span, 8), span)]
@@ -172,7 +186,8 @@
     tell(1)
     for n in range(chunks):
         local_load(load_of_pair(n)).wait()
-        pair_copy(n).start()
+        for p in range(pieces(n)):
+            pair_copy(n, p).start()
     transpose(0)
     for dz in away:
         send_ids(ids.at[x, z], device(0, dz, 0), 0)
@@ -279,7 +294,8 @@
     pltpu.make_async_copy(x_rest, x_rest, x_send).wait()
     pltpu.make_async_copy(z_rest, z_rest, z_send).wait()
     for n in range(chunks):
-        pair_copy(n).wait_send()
+        for p in range(pieces(n)):
+            pair_copy(n, p).wait_send()
 
 
 def write_out(table_ref, pooled_ref, table_out, pooled_out, sems):
@@ -318,7 +334,7 @@
             pltpu.VMEM((zn, 2, 8, LANES), f32),
             pltpu.VMEM((zn * 2, 8, LANES), f32),
             pltpu.SMEM((xn, zn, 4, LANES), jnp.int32),
-            dma((chunks,)), dma((chunks,)), dma((chunks,)),
+            dma((chunks,)), dma((chunks + 3,)), dma((chunks + 3,)),
             dma((2,)), dma((2,)), dma, dma, dma, dma, dma, dma, dma, dma, dma,
             pltpu.SemaphoreType.REGULAR((chunks // 4 + xn // 2,)),
         ],

time: 61.4 us -> 61.2 us (level)
  no operation moved by 1% of the time
where the time goes in v9:
time: 61.2 us; the launch traced here: 60.4 us
  Pallas kernels  59.8 us (98%)
  between operations  0.64 us (1%)
    pallas_call x1, Pallas kernels, per_device(): pl.pallas_call(functools.partial(kernel, zn, xn, span), out_shape=[pltpu....  58.4 us
    pallas_call x1, Pallas kernels, per_device(): pl.pallas_call(write_out, out_shape=[jax.ShapeDtypeStruct(row_table.shape...  1.34 us

profile of v9, /device:TPU:1, one launch (start us, length us, event | category | flops | bytes accessed | tf_op | source)
XLA Modules:
  0.0 60.4 jit_solution(10927972949089617190)
XLA Ops:
  0.6 58.4 %shard_map.41 = (f32[32,32,512]{2,1,0:T(8,128)S(1)}, f32[32,64]{1,0:T(8,128)S(1)}) custom-call(f32[64,8192]{1,0:T(8,128)} %bitcast.1, s32[32,32]{1,0:T(8,128)} %bags_ref.1), custom_call_target="tpu_custom_call" | custom-call | tf_op jit(solution)/shard_map/pallas_call | solution.py:317
  59.1 1.3 %shard_map.42 = (f32[32,32,512]{2,1,0:T(8,128)}, f32[32,64]{1,0:T(8,128)}) custom-call(f32[32,32,512]{2,1,0:T(8,128)S(1)} %get-tuple-element.4.table_ref, f32[32,64]{1,0:T(8,128)S(1)} %get-tuple-element.5.pooled_ref), custom_call_target="tpu_custom_call" | custom-call | tf_op jit(solution)/shard_map/pallas_call | solution.py:343

commit v10 on v9

--- a/solution.py
+++ b/solution.py
@@ -180,7 +180,7 @@
     last = [c for c in quad if hops_to(*c) == 1]
     reached = [[c for c in columns if c not in quad and hops_to(*c) == n] for n in range(rounds + 1)]
     reached[rounds] += [c for c in quad if hops_to(*c) == 2]
-    long_hops, short_hops = away[: (zn - 1) // 2], away[(zn - 1) // 2 :]
+    long_hops, short_hops = away[: zn // 2], away[zn // 2 :]
 
     pl.semaphore_wait(barrier, zn + len(beside))
     tell(1)
@@ -262,7 +262,7 @@
         total = total + x_in[lax.rem(x + d, xn)]
     held[...] = total
 
-    for d in range(zn):
+    for d in away + [0]:
         zz = lax.rem(z + d, zn)
         for e in range(2):
             if d == 0 and e == 0:

time: 61.2 us -> 60.9 us (level); the launches traced: 60.4 us -> 60.8 us
  no operation moved by 1% of the time
where the time goes in v10:
time: 60.9 us; the launch traced here: 60.8 us
  Pallas kernels  60.2 us (99%)
  between operations  0.64 us (1%)
    pallas_call x1, Pallas kernels, per_device(): pl.pallas_call(functools.partial(kernel, zn, xn, span), out_shape=[pltpu....  58.9 us
    pallas_call x1, Pallas kernels, per_device(): pl.pallas_call(write_out, out_shape=[jax.ShapeDtypeStruct(row_table.shape...  1.34 us

profile of v10, /device:TPU:1, one launch (start us, length us, event | category | flops | bytes accessed | tf_op | source)
XLA Modules:
  0.0 60.8 jit_solution(17796880308015094266)
XLA Ops:
  0.6 58.9 %shard_map.41 = (f32[32,32,512]{2,1,0:T(8,128)S(1)}, f32[32,64]{1,0:T(8,128)S(1)}) custom-call(f32[64,8192]{1,0:T(8,128)} %bitcast.1, s32[32,32]{1,0:T(8,128)} %bags_ref.1), custom_call_target="tpu_custom_call" | custom-call | tf_op jit(solution)/shard_map/pallas_call | solution.py:317
  59.5 1.3 %shard_map.42 = (f32[32,32,512]{2,1,0:T(8,128)}, f32[32,64]{1,0:T(8,128)}) custom-call(f32[32,32,512]{2,1,0:T(8,128)S(1)} %get-tuple-element.4.table_ref, f32[32,64]{1,0:T(8,128)S(1)} %get-tuple-element.5.pooled_ref), custom_call_target="tpu_custom_call" | custom-call | tf_op jit(solution)/shard_map/pallas_call | solution.py:343
